TPU v7x, 32 devices: a whole 2x2x4 slice. The times are simulated.
32 devices in a mesh: own: 8 (over z, x), rep: 4 (over y, core).
Axes of the slice: x: 2, y: 2, z: 4, core: 2. Of those that a mesh axis runs over, the one named last changes fastest.
Arguments:
- block_pool: bfloat16 [2048, 64, 576], P(('own', 'rep')), may hold values from -16 to 16
- sel_index: int32 [1024], P(('own', 'rep')), may hold values from 0 to 63
- sel_layer: int32 [1024], P(('own', 'rep')), may hold values from 0 to 3, as said below
- counts: int32 [32], P(('own', 'rep')), may hold values from 8 to 32, as said below
Outputs:
- quant_codes: bfloat16 [8, 4, 8, 8, 18432], P('own', 'rep')
- quant_steps: float32 [8, 288], P('own')
- clip_error: float32 [8, 288], P('own')
Inputs may be any that keep to these rules, and one draw needn't show every extreme that they name: `sel_layer`: among the 32 entries of one device, at most 8 name any one layer; the first 8 entries of every device all name one and the same layer. `counts`: some device has all 32 entries live.
All inputs are finite; a program needn't handle non-finite values.
Results may differ from a plain program's by a relative error of at most 0.001.
Values may be sent and summed in bfloat16 or wider, within the bound.
A program may use at most 128 MiB of HBM per device.

v0:
```python
import functools
import math

import jax
import jax.numpy as jnp
from jax import lax
from jax.experimental import pallas as pl
from jax.experimental.pallas import tpu as pltpu
from jax.sharding import PartitionSpec as P

SLICES = 2
LANES = 128
headroom = 0.5


def partner_layer(my_layer, layers, k):
    near = layers // 2
    if k < near:
        return lax.rem(my_layer + k, near) + (1 - my_layer // near) * near
    return lax.rem(my_layer + 1 + k - near, near) + (my_layer // near) * near


def send_order(layers):
    straight, across, both = range(1), range(1, SLICES), range(SLICES)
    own = [(layers - 1, across)]
    near = [(k, both) for k in range(layers // 2, layers - 1)]
    far = [(k, part) for k in range(1, layers // 2) for part in (across, straight)]
    return [(0, across), (0, straight)] + near + far + own


def fill_slots(live, index_row, layer_row, table, layers, cap, empty):
    n_select = index_row.shape[1]
    is_live = lax.broadcasted_iota(jnp.int32, (1, n_select), 1) < live
    before = lax.broadcasted_iota(jnp.int32, (n_select, n_select), 0)
    after = lax.broadcasted_iota(jnp.int32, (n_select, n_select), 1)
    earlier = jnp.where(before < after, 1.0, 0.0)
    wanted = lax.broadcasted_iota(jnp.int32, (layers, n_select), 0)
    matches = jnp.where((layer_row == wanted) & is_live, 1.0, 0.0)
    ranking = jnp.dot(matches, earlier, preferred_element_type=jnp.float32)
    slot = lax.broadcasted_iota(jnp.int32, (cap, n_select), 0).astype(jnp.float32)
    shifted = index_row.astype(jnp.float32) - float(empty)
    for layer in range(layers):
        hit = (ranking[layer:layer + 1] == slot) & (matches[layer:layer + 1] > 0.5)
        found = jnp.sum(jnp.where(hit, shifted, 0.0), axis=1, keepdims=True) + float(empty)
        table[layer * cap:(layer + 1) * cap, :] = jnp.broadcast_to(found, (cap, LANES)).astype(jnp.int32)


def kernel(own_n, rep_n, cap, live_ref, index_ref, layer_ref, pool_ref, codes_ref, steps_ref, err_ref,
           table, slots, pool_v, stage, send, recv, pk_send, pk_recv, pk_mine, pk_rep, er_mine, er_rep,
           table_sem, pool_sem, ssem, rsem, pssem, prsem, rpssem, rprsem, ressem, rersem):
    rows, tokens, width = pool_ref.shape
    half = width // SLICES
    flat = tokens * half
    group = LANES // math.gcd(half, LANES)
    period = group * half
    layers = own_n // SLICES
    me = lax.axis_index("own")
    rep = lax.axis_index("rep")
    my_layer = me // SLICES
    my_slice = me % SLICES
    tiles = stage.shape[0]
    denominator = float(own_n * rep_n * cap * tokens)
    pieces = pool_sem.shape[0]
    per_piece = rows // pieces

    loads = [
        pltpu.make_async_copy(
            pool_ref.at[pl.ds(p * per_piece, per_piece)],
            pool_v.at[pl.ds(p * per_piece, per_piece)],
            pool_sem.at[p],
        )
        for p in range(pieces)
    ]
    for load in loads:
        load.start()

    barrier = pltpu.get_barrier_semaphore()
    for k in range(1, own_n):
        pl.semaphore_signal(barrier, inc=1, device_id={"own": lax.rem(me + k, own_n)},
                            device_id_type=pl.DeviceIdType.MESH)
    for k in range(1, rep_n):
        pl.semaphore_signal(barrier, inc=1, device_id={"rep": lax.rem(rep + k, rep_n)},
                            device_id_type=pl.DeviceIdType.MESH)

    pool_v[rows] = jnp.zeros((tokens, width), pool_v.dtype)
    fill_slots(live_ref[0], index_ref[...], layer_ref[...], table, layers, cap, rows)
    to_scalars = pltpu.make_async_copy(table, slots, table_sem)
    to_scalars.start()
    to_scalars.wait()
    for load in loads:
        load.wait()

    def row_of(slot):
        return jnp.minimum(jnp.maximum(slots[slot, 0], 0), rows)

    def layer_peak(layer, carry):
        best = jnp.zeros((tokens, width), pool_v.dtype)
        for c in range(cap):
            best = jnp.maximum(best, jnp.abs(pool_v[row_of(layer * cap + c)]))
        top = jnp.max(best.astype(jnp.float32), axis=0, keepdims=True)
        for part in range(SLICES):
            one = top[:, part * half:(part + 1) * half]
            pk_send[layer * SLICES + part] = jnp.concatenate([one] * group, axis=1)
        return carry

    def peak_copy(peer, landing):
        return pltpu.make_async_remote_copy(
            src_ref=pk_send.at[peer], dst_ref=pk_recv.at[landing],
            send_sem=pssem.at[peer], recv_sem=prsem.at[landing],
            device_id={"own": peer}, device_id_type=pl.DeviceIdType.MESH)

    def block_copy(peer, landing):
        return pltpu.make_async_remote_copy(
            src_ref=send.at[peer], dst_ref=recv.at[landing],
            send_sem=ssem.at[peer], recv_sem=rsem.at[landing],
            device_id={"own": peer}, device_id_type=pl.DeviceIdType.MESH)

    def flatten_layer(layer):
        for c in range(cap):
            block = pool_v[row_of(layer * cap + c)].astype(jnp.float32)
            for q in range(tiles):
                lo, hi = q * LANES, min(width, (q + 1) * LANES)
                stage[q, c * tokens:(c + 1) * tokens, 0:hi - lo] = block[:, lo:hi]

        def flatten(i, carry):
            rows_of = [
                jnp.concatenate(
                    [stage[q, pl.ds(i * group + j, cap, stride=tokens), :] for q in range(tiles)], axis=1)
                for j in range(group)
            ]
            for part in range(SLICES):
                joined = jnp.concatenate([r[:, part * half:(part + 1) * half] for r in rows_of], axis=1)
                at = pl.multiple_of(i * period, period)
                send[layer * SLICES + part, :, pl.ds(at, period)] = joined.astype(send.dtype)
            return carry

        lax.fori_loop(0, tokens // group, flatten, 0)

    def start_blocks(layer, parts):
        for part in parts:
            block_copy(layer * SLICES + lax.rem(my_slice + part, SLICES), me).start()

    flattened = set()
    for place, (k, parts) in enumerate(send_order(layers)):
        layer = partner_layer(my_layer, layers, k)
        if k not in flattened:
            flatten_layer(layer)
            flattened.add(k)
        if not place:
            pl.semaphore_wait(barrier, own_n - 1 + rep_n - 1)
        for part in parts:
            block_copy(layer * SLICES + lax.rem(my_slice + part, SLICES), me).start()
        if place == 1:
            lax.fori_loop(0, layers, layer_peak, 0)
            for step in range(1, own_n):
                peak_copy(lax.rem(me + step, own_n), me).start()

    best = pk_send[me]
    for k in range(1, own_n):
        src = lax.rem(me + k, own_n)
        peak_copy(src, src).wait_recv()
        best = jnp.maximum(best, pk_recv[src])
    pk_mine[...] = best

    def rep_copy(mine, table, s_sem, r_sem, peer, landing):
        return pltpu.make_async_remote_copy(
            src_ref=mine, dst_ref=table.at[landing],
            send_sem=s_sem.at[peer], recv_sem=r_sem.at[landing],
            device_id={"rep": peer}, device_id_type=pl.DeviceIdType.MESH)

    for k in range(1, rep_n):
        rep_copy(pk_mine, pk_rep, rpssem, rprsem, lax.rem(rep + k, rep_n), rep).start()
    for k in range(1, rep_n):
        src = lax.rem(rep + k, rep_n)
        rep_copy(pk_mine, pk_rep, rpssem, rprsem, src, src).wait_recv()
        best = jnp.maximum(best, pk_rep[src])

    step = headroom * jnp.maximum(best, 1.0) / 127.0
    inverse = 1.0 / step
    steps_ref[...] = step[:, :half]
    step_wide = jnp.broadcast_to(step, (cap, period))
    inv_wide = jnp.broadcast_to(inverse, (cap, period))

    def encode(source, src, total):
        def one(i, total):
            at = pl.multiple_of(i * period, period)
            x = source[src, :, pl.ds(at, period)].astype(jnp.float32)
            y = jnp.clip(x * inv_wide, -127.0, 127.0).astype(codes_ref.dtype)
            codes_ref[0, 0, src, :, pl.ds(at, period)] = y
            diff = x - y.astype(jnp.float32) * step_wide
            return total + diff * diff
        return lax.fori_loop(0, tokens // group, one, total)

    total = encode(send, me, jnp.zeros((cap, period), jnp.float32))
    for part in range(1, SLICES):
        src = my_layer * SLICES + lax.rem(my_slice + part, SLICES)
        block_copy(src, src).wait_recv()
        total = encode(recv, src, total)
    for k in list(range(layers // 2, layers - 1)) + list(range(layers // 2)):
        layer = partner_layer(my_layer, layers, k)
        for part in range(SLICES):
            src = layer * SLICES + lax.rem(my_slice + part, SLICES)
            block_copy(src, src).wait_recv()
            total = encode(recv, src, total)

    mine = jnp.sum(total, axis=0, keepdims=True)
    er_mine[...] = mine
    for k in range(1, rep_n):
        rep_copy(er_mine, er_rep, ressem, rersem, lax.rem(rep + k, rep_n), rep).start()
    er_rep[rep] = mine
    for k in range(1, rep_n):
        src = lax.rem(rep + k, rep_n)
        rep_copy(er_mine, er_rep, ressem, rersem, src, src).wait_recv()
    whole = er_rep[0]
    for k in range(1, rep_n):
        whole = whole + er_rep[k]
    folded = whole[:, :half]
    for j in range(1, group):
        folded = folded + whole[:, j * half:(j + 1) * half]
    narrow = step[:, :half]
    err_ref[...] = folded / (narrow * narrow * denominator)

    for k in range(1, own_n):
        peer = lax.rem(me + k, own_n)
        peak_copy(peer, me).wait_send()
        block_copy(peer, me).wait_send()
    for k in range(1, rep_n):
        peer = lax.rem(rep + k, rep_n)
        rep_copy(pk_mine, pk_rep, rpssem, rprsem, peer, rep).wait_send()
        rep_copy(er_mine, er_rep, ressem, rersem, peer, rep).wait_send()


def write_out(codes_v, steps_v, err_v, codes_ref, steps_ref, err_ref, sems):
    own_n = codes_v.shape[2]
    moves = [pltpu.make_async_copy(codes_v.at[0, 0, src], codes_ref.at[0, 0, src], sems.at[src])
             for src in range(own_n)]
    moves.append(pltpu.make_async_copy(steps_v, steps_ref, sems.at[own_n]))
    moves.append(pltpu.make_async_copy(err_v, err_ref, sems.at[own_n + 1]))
    for move in moves:
        move.start()
    for move in moves:
        move.wait()


def body(block_pool, sel_index, sel_layer, counts):
    own_n = lax.axis_size("own")
    rep_n = lax.axis_size("rep")
    cap = sel_index.shape[0] // 4
    rows, tokens, width = block_pool.shape
    half = width // SLICES
    flat = tokens * half
    group = LANES // math.gcd(half, LANES)
    period = group * half
    layers = own_n // SLICES
    f32 = jnp.float32
    dma = pltpu.SemaphoreType.DMA
    dtype = block_pool.dtype
    codes, steps, err = pl.pallas_call(
        functools.partial(kernel, own_n, rep_n, cap),
        out_shape=(
            pltpu.VMEM((1, 1, own_n, cap, flat), dtype),
            pltpu.VMEM((1, half), f32),
            pltpu.VMEM((1, half), f32),
        ),
        in_specs=[
            pl.BlockSpec(memory_space=pltpu.SMEM), pl.BlockSpec(memory_space=pltpu.VMEM),
            pl.BlockSpec(memory_space=pltpu.VMEM), pl.BlockSpec(memory_space=pltpu.HBM)],
        out_specs=(
            pl.BlockSpec(memory_space=pltpu.VMEM),
            pl.BlockSpec(memory_space=pltpu.VMEM),
            pl.BlockSpec(memory_space=pltpu.VMEM),
        ),
        scratch_shapes=[
            pltpu.VMEM((layers * cap, LANES), jnp.int32),
            pltpu.SMEM((layers * cap, LANES), jnp.int32),
            pltpu.VMEM((rows + 1, tokens, width), dtype),
            pltpu.VMEM((pl.cdiv(width, LANES), cap * tokens, LANES), f32),
            pltpu.VMEM((own_n, cap, flat), dtype),
            pltpu.VMEM((own_n, cap, flat), dtype),
            pltpu.VMEM((own_n, 1, period), f32),
            pltpu.VMEM((own_n, 1, period), f32),
            pltpu.VMEM((1, period), f32),
            pltpu.VMEM((rep_n, 1, period), f32),
            pltpu.VMEM((1, period), f32),
            pltpu.VMEM((rep_n, 1, period), f32),
            dma, dma((8,)),
            dma((own_n,)), dma((own_n,)), dma((own_n,)), dma((own_n,)),
            dma((rep_n,)), dma((rep_n,)), dma((rep_n,)), dma((rep_n,)),
        ],
        compiler_params=pltpu.CompilerParams(
            collective_id=0, has_side_effects=True, vmem_limit_bytes=(63 * 1024 * 1024 - own_n * cap * flat * 2)),
        name="latent_code",
    )(counts, sel_index[None], sel_layer[None], block_pool)
    hbm = pl.BlockSpec(memory_space=pltpu.HBM)
    return pl.pallas_call(
        write_out,
        out_shape=tuple(jax.ShapeDtypeStruct(x.shape, x.dtype) for x in (codes, steps, err)),
        in_specs=[pl.BlockSpec(memory_space=pltpu.VMEM)] * 3,
        out_specs=(hbm, hbm, hbm),
        scratch_shapes=[dma((own_n + 2,))],
        compiler_params=pltpu.CompilerParams(vmem_limit_bytes=4 * 1024 * 1024),
        name="write_out",
    )(codes, steps, err)


def solution(mesh):
    return jax.shard_map(
        body,
        mesh=mesh,
        in_specs=(
            P(("own", "rep"), None, None),
            P(("own", "rep")),
            P(("own", "rep")),
            P(("own", "rep")),
        ),
        out_specs=(P("own", "rep", None, None, None), P("own", None), P("own", None)),
        check_vma=False,
    )
```

profile of v0, /device:TPU:8, one launch (start us, length us, event | category | flops | bytes accessed | tf_op | source)
XLA Modules:
  0.0 65.9 jit_solution(3241313238759892389)
XLA Ops:
  1.3 63.1 %latent_code.1 = (bf16[1,1,8,8,18432]{4,3,2,1,0:T(8,128)(2,1)S(1)}, f32[1,288]{1,0:T(1,128)S(1)}, f32[1,288]{1,0:T(1,128)S(1)}) custom-call(s32[1]{0:T(128)S(6)} %copy.7.live_ref, s32[1,32]{1,0:T(1,128)} %bitcast.2, s32[1,32]{1,0:T(1,128)} %bitcast.3, bf16[64,64,576]{2,1,0:T(8,128)(2,1)} %pool_ref.1), custom_call_target="tpu_custom_call" | custom-call | tf_op jit(solution)/shard_map/latent_code/pallas_call | solution.py:258
  64.4 1.5 %write_out.1 = (bf16[1,1,8,8,18432]{4,3,2,1,0:T(8,128)(2,1)}, f32[1,288]{1,0:T(1,128)}, f32[1,288]{1,0:T(1,128)}) custom-call(bf16[1,1,8,8,18432]{4,3,2,1,0:T(8,128)(2,1)S(1)} %get-tuple-element.6.codes_v, f32[1,288]{1,0:T(1,128)S(1)} %get-tuple-element.7.steps_v, f32[1,288]{1,0:T(1,128)S(1)} %get-tuple-element.8.err_v), custom_call_target="tpu_custom_call" | custom-call | tf_op jit(solution)/shard_map/write_out/pallas_call | solution.py:295
where the time goes:
time: 66.3 us; the launch traced here: 65.9 us
  Pallas kernels  64.6 us (97%)
  between operations  1.29 us (2%)
    pallas_call x1, Pallas kernels, body(): pl.pallas_call(functools.partial(kernel, own_n, rep_n, cap), out_shape=(p...  63.1 us
    pallas_call x1, Pallas kernels, body(): pl.pallas_call(write_out, out_shape=tuple((jax.ShapeDtypeStruct(x.shape,...  1.49 us

commit v1 on v0

v1 whole, which is shorter than its diff:
```python
import functools
import math

import jax
import jax.numpy as jnp
from jax import lax
from jax.experimental import pallas as pl
from jax.experimental.pallas import tpu as pltpu
from jax.sharding import PartitionSpec as P

SLICES = 2
LANES = 128
headroom = 0.5


def ring_place(layer, layers):
    odd = layer % 2
    return odd * ((layer + 1) // 2) + (1 - odd) * lax.rem(layers - layer // 2, layers)


def ring_layer(place, layers):
    near = jnp.maximum(2 * place - 1, 0)
    return jnp.where(place <= layers // 2, near, 2 * (layers - place))


def partner_layer(my_layer, layers, k):
    return ring_layer(lax.rem(ring_place(my_layer, layers) + k, layers), layers)


def fill_slots(live, index_row, layer_row, table, layers, cap, empty):
    n_select = index_row.shape[1]
    is_live = lax.broadcasted_iota(jnp.int32, (1, n_select), 1) < live
    before = lax.broadcasted_iota(jnp.int32, (n_select, n_select), 0)
    after = lax.broadcasted_iota(jnp.int32, (n_select, n_select), 1)
    earlier = jnp.where(before < after, 1.0, 0.0)
    wanted = lax.broadcasted_iota(jnp.int32, (layers, n_select), 0)
    matches = jnp.where((layer_row == wanted) & is_live, 1.0, 0.0)
    ranking = jnp.dot(matches, earlier, preferred_element_type=jnp.float32)
    slot = lax.broadcasted_iota(jnp.int32, (cap, n_select), 0).astype(jnp.float32)
    shifted = index_row.astype(jnp.float32) - float(empty)
    for layer in range(layers):
        hit = (ranking[layer:layer + 1] == slot) & (matches[layer:layer + 1] > 0.5)
        found = jnp.sum(jnp.where(hit, shifted, 0.0), axis=1, keepdims=True) + float(empty)
        table[layer * cap:(layer + 1) * cap, :] = jnp.broadcast_to(found, (cap, LANES)).astype(jnp.int32)


def kernel(own_n, rep_n, cap, live_hbm, index_hbm, layer_hbm, pool_ref, codes_ref, steps_ref, err_ref,
           live_v, index_v, layer_v, table, slots, pool_v, stage, send, recv,
           pk_send, pk_recv, pk_mine, pk_rep, st_mine, st_recv, pe_send, pe_recv, er_mine, er_rep,
           small_sem, table_sem, pool_sem, ssem, rsem, pssem, prsem, rpssem, rprsem, tssem, trsem,
           essem, ersem, ressem, rersem):
    rows, tokens, width = pool_ref.shape
    half = width // SLICES
    group = LANES // math.gcd(half, LANES)
    period = group * half
    loops = tokens // group
    layers = own_n // SLICES
    me = lax.axis_index("own")
    rep = lax.axis_index("rep")
    my_layer = me // SLICES
    my_slice = me % SLICES
    tiles = stage.shape[0]
    denominator = float(own_n * rep_n * cap * tokens)
    pieces = pool_sem.shape[0]
    per_piece = rows // pieces
    f32 = jnp.float32

    barrier = pltpu.get_barrier_semaphore()
    for k in range(1, own_n):
        pl.semaphore_signal(barrier, inc=1, device_id={"own": lax.rem(me + k, own_n)},
                            device_id_type=pl.DeviceIdType.MESH)
    for k in range(1, rep_n):
        pl.semaphore_signal(barrier, inc=1, device_id={"rep": lax.rem(rep + k, rep_n)},
                            device_id_type=pl.DeviceIdType.MESH)

    smalls = [pltpu.make_async_copy(a, b, small_sem.at[i])
              for i, (a, b) in enumerate(((live_hbm, live_v), (index_hbm, index_v), (layer_hbm, layer_v)))]
    for small in smalls:
        small.start()
    loads = [
        pltpu.make_async_copy(
            pool_ref.at[pl.ds(p * per_piece, per_piece)],
            pool_v.at[pl.ds(p * per_piece, per_piece)],
            pool_sem.at[p],
        )
        for p in range(pieces)
    ]
    for load in loads:
        load.start()

    pool_v[rows] = jnp.zeros((tokens, width), pool_v.dtype)
    for small in smalls:
        small.wait()
    fill_slots(live_v[...], index_v[...], layer_v[...], table, layers, cap, rows)
    to_scalars = pltpu.make_async_copy(table, slots, table_sem)
    to_scalars.start()
    to_scalars.wait()
    for load in loads:
        load.wait()

    def row_of(slot):
        return jnp.minimum(jnp.maximum(slots[slot, 0], 0), rows)

    def layer_peak(layer, carry):
        best = jnp.zeros((tokens, width), pool_v.dtype)
        for c in range(cap):
            best = jnp.maximum(best, jnp.abs(pool_v[row_of(layer * cap + c)]))
        top = jnp.max(best.astype(f32), axis=0, keepdims=True)
        for part in range(SLICES):
            pk_send[layer * SLICES + part] = top[:, part * half:(part + 1) * half]
        return carry

    def own_copy(src, dst, s_sem, r_sem, peer):
        return pltpu.make_async_remote_copy(
            src_ref=src, dst_ref=dst, send_sem=s_sem, recv_sem=r_sem,
            device_id={"own": peer}, device_id_type=pl.DeviceIdType.MESH)

    def rep_copy(mine, table, s_sem, r_sem, peer, landing):
        return pltpu.make_async_remote_copy(
            src_ref=mine, dst_ref=table.at[landing],
            send_sem=s_sem.at[peer], recv_sem=r_sem.at[landing],
            device_id={"rep": peer}, device_id_type=pl.DeviceIdType.MESH)

    def peak_copy(peer, landing):
        return own_copy(pk_send.at[peer], pk_recv.at[landing], pssem.at[peer], prsem.at[landing], peer)

    def step_copy(peer, landing):
        return own_copy(st_mine, st_recv.at[landing], tssem.at[peer], trsem.at[landing], peer)

    def part_error_copy(peer, landing):
        return own_copy(pe_send.at[peer], pe_recv.at[landing], essem.at[peer], ersem.at[landing], peer)

    quarter = loops // 4
    first, middle, rest = (0, quarter, 0), (quarter, loops - 2 * quarter, 1), (loops - quarter, quarter, 2)
    all_cols = (0, loops, 0)

    def block_copy(peer, landing, cols, into):
        lanes = pl.ds(cols[0] * period, cols[1] * period)
        to = into.at[0, 0] if len(into.shape) == 5 else into
        return own_copy(send.at[peer, :, lanes], to.at[landing, :, lanes],
                        ssem.at[peer, cols[2]], rsem.at[landing, cols[2]], peer)

    def flatten_layer(layer, cols):
        start, count, _ = cols
        t0, t1 = start * group, (start + count) * group
        for c in range(cap):
            block = pool_v[row_of(layer * cap + c), t0:t1, :].astype(f32)
            for q in range(tiles):
                lo, hi = q * LANES, min(width, (q + 1) * LANES)
                stage[q, c * tokens + t0:c * tokens + t1, 0:hi - lo] = block[:, lo:hi]

        def flatten(i, carry):
            rows_of = [
                jnp.concatenate(
                    [stage[q, pl.ds(i * group + j, cap, stride=tokens), :] for q in range(tiles)], axis=1)
                for j in range(group)
            ]
            for part in range(SLICES):
                joined = jnp.concatenate([r[:, part * half:(part + 1) * half] for r in rows_of], axis=1)
                at = pl.multiple_of(i * period, period)
                send[layer * SLICES + part, :, pl.ds(at, period)] = joined.astype(send.dtype)
            return carry

        lax.fori_loop(start, start + count, flatten, 0)

    def owner(layer, part):
        return layer * SLICES + lax.rem(my_slice + part, SLICES)

    across_first = list(range(1, SLICES)) + [0]
    order = [k for k in range(1, layers) if k != layers // 2]
    last = partner_layer(my_layer, layers, layers // 2)
    to_layer = [partner_layer(my_layer, layers, k) for k in order]
    from_layer = [partner_layer(my_layer, layers, layers - k) for k in order]

    def send_blocks(layer, cols):
        for part in across_first:
            block_copy(owner(layer, part), me, cols, recv).start()

    lax.fori_loop(0, layers, layer_peak, 0)
    flatten_layer(to_layer[0], first)
    pl.semaphore_wait(barrier, own_n - 1 + rep_n - 1)
    for k in range(1, own_n):
        peer = lax.rem(me + k, own_n)
        peak_copy(peer, me).start()
    send_blocks(to_layer[0], first)
    flatten_layer(to_layer[0], middle)
    send_blocks(to_layer[0], middle)
    flatten_layer(to_layer[0], rest)

    best = pk_send[me]
    for k in range(1, own_n):
        src = lax.rem(me + k, own_n)
        peak_copy(src, src).wait_recv()
        best = jnp.maximum(best, pk_recv[src])
    pk_mine[...] = best
    for k in range(1, rep_n):
        rep_copy(pk_mine, pk_rep, rpssem, rprsem, lax.rem(rep + k, rep_n), rep).start()
    flatten_layer(last, all_cols)
    for k in range(1, rep_n):
        src = lax.rem(rep + k, rep_n)
        rep_copy(pk_mine, pk_rep, rpssem, rprsem, src, src).wait_recv()
        best = jnp.maximum(best, pk_rep[src])

    step = headroom * jnp.maximum(best, 1.0) / 127.0
    steps_ref[...] = step
    st_mine[...] = step
    for part in across_first:
        step_copy(owner(last, part), me).start()
    send_blocks(to_layer[0], rest)
    for i, layer in enumerate(to_layer[1:]):
        flatten_layer(layer, all_cols)
        send_blocks(layer, all_cols)
    flatten_layer(my_layer, all_cols)
    for part in range(1, SLICES):
        block_copy(owner(my_layer, part), me, all_cols, recv).start()

    def wide(row):
        return jnp.broadcast_to(jnp.concatenate([row] * group, axis=1), (cap, period))

    def encode(source, target, src, one_step, total):
        step_wide = wide(one_step)
        inv_wide = wide(1.0 / one_step)

        def one(i, total):
            lanes = pl.ds(pl.multiple_of(i * period, period), period)
            x = source[src, :, lanes].astype(f32)
            y = jnp.clip(x * inv_wide, -127.0, 127.0).astype(codes_ref.dtype)
            target[src, :, lanes] = y
            diff = x - y.astype(f32) * step_wide
            return total + diff * diff
        return lax.fori_loop(0, loops, one, total)

    def fold(total):
        row = jnp.sum(total, axis=0, keepdims=True)
        folded = row[:, :half]
        for j in range(1, group):
            folded = folded + row[:, j * half:(j + 1) * half]
        return folded

    zero = jnp.zeros((cap, period), f32)
    codes_at = codes_ref.at[0, 0]
    total = encode(send, codes_at, me, step, zero)

    for part in across_first:
        peer = owner(last, part)
        step_copy(peer, peer).wait_recv()
        pe_send[peer] = fold(encode(send, send, peer, st_recv[peer], zero))
        part_error_copy(peer, me).start()
        block_copy(peer, me, all_cols, codes_ref).start()

    for part in across_first:
        src = owner(from_layer[0], part)
        for cols in (first, middle, rest):
            block_copy(src, src, cols, recv).wait_recv()
        total = encode(recv, codes_at, src, step, total)
    for part in range(1, SLICES):
        src = owner(my_layer, part)
        block_copy(src, src, all_cols, recv).wait_recv()
        total = encode(recv, codes_at, src, step, total)
    for i, layer in enumerate(from_layer[1:]):
        for part in across_first:
            src = owner(layer, part)
            block_copy(src, src, all_cols, recv).wait_recv()
            total = encode(recv, codes_at, src, step, total)

    mine = fold(total)
    for part in across_first:
        src = owner(last, part)
        part_error_copy(src, src).wait_recv()
        mine = mine + pe_recv[src]
    er_mine[...] = mine
    for k in range(1, rep_n):
        rep_copy(er_mine, er_rep, ressem, rersem, lax.rem(rep + k, rep_n), rep).start()
    er_rep[rep] = mine
    for k in range(1, rep_n):
        src = lax.rem(rep + k, rep_n)
        rep_copy(er_mine, er_rep, ressem, rersem, src, src).wait_recv()
    whole = er_rep[0]
    for k in range(1, rep_n):
        whole = whole + er_rep[k]
    err_ref[...] = whole / (step * step * denominator)

    for k in range(1, own_n):
        peak_copy(lax.rem(me + k, own_n), me).wait_send()
    for k in range(1, rep_n):
        peer = lax.rem(rep + k, rep_n)
        rep_copy(pk_mine, pk_rep, rpssem, rprsem, peer, rep).wait_send()
        rep_copy(er_mine, er_rep, ressem, rersem, peer, rep).wait_send()
    for part in across_first:
        step_copy(owner(last, part), me).wait_send()
        part_error_copy(owner(last, part), me).wait_send()
        for cols in (first, middle, rest):
            block_copy(owner(to_layer[0], part), me, cols, recv).wait_send()
        for layer in to_layer[1:]:
            block_copy(owner(layer, part), me, all_cols, recv).wait_send()
    for part in range(1, SLICES):
        block_copy(owner(my_layer, part), me, all_cols, recv).wait_send()
    for part in across_first:
        peer = owner(last, part)
        block_copy(peer, me, all_cols, codes_ref).wait_send()
        block_copy(peer, peer, all_cols, codes_ref).wait_recv()


def write_out(codes_v, steps_v, err_v, codes_ref, steps_ref, err_ref, sems):
    own_n = codes_v.shape[2]
    moves = [pltpu.make_async_copy(codes_v.at[0, 0, src], codes_ref.at[0, 0, src], sems.at[src])
             for src in range(own_n)]
    moves.append(pltpu.make_async_copy(steps_v, steps_ref, sems.at[own_n]))
    moves.append(pltpu.make_async_copy(err_v, err_ref, sems.at[own_n + 1]))
    for move in moves:
        move.start()
    for move in moves:
        move.wait()


def body(block_pool, sel_index, sel_layer, counts):
    own_n = lax.axis_size("own")
    rep_n = lax.axis_size("rep")
    cap = sel_index.shape[0] // 4
    rows, tokens, width = block_pool.shape
    n_select = sel_index.shape[0]
    half = width // SLICES
    flat = tokens * half
    layers = own_n // SLICES
    f32, i32 = jnp.float32, jnp.int32
    dma = pltpu.SemaphoreType.DMA
    dtype = block_pool.dtype
    hbm = pl.BlockSpec(memory_space=pltpu.HBM)
    vmem = pl.BlockSpec(memory_space=pltpu.VMEM)
    codes, steps, err = pl.pallas_call(
        functools.partial(kernel, own_n, rep_n, cap),
        out_shape=(
            pltpu.VMEM((1, 1, own_n, cap, flat), dtype),
            pltpu.VMEM((1, half), f32),
            pltpu.VMEM((1, half), f32),
        ),
        in_specs=[hbm] * 4,
        out_specs=(vmem,) * 3,
        scratch_shapes=[
            pltpu.VMEM((1, 1), i32), pltpu.VMEM((1, n_select), i32), pltpu.VMEM((1, n_select), i32),
            pltpu.VMEM((layers * cap, LANES), i32),
            pltpu.SMEM((layers * cap, LANES), i32),
            pltpu.VMEM((rows + 1, tokens, width), dtype),
            pltpu.VMEM((pl.cdiv(width, LANES), cap * tokens, LANES), f32),
            pltpu.VMEM((own_n, cap, flat), dtype),
            pltpu.VMEM((own_n, cap, flat), dtype),
            pltpu.VMEM((own_n, 1, half), f32), pltpu.VMEM((own_n, 1, half), f32),
            pltpu.VMEM((1, half), f32), pltpu.VMEM((rep_n, 1, half), f32),
            pltpu.VMEM((1, half), f32), pltpu.VMEM((own_n, 1, half), f32),
            pltpu.VMEM((own_n, 1, half), f32), pltpu.VMEM((own_n, 1, half), f32),
            pltpu.VMEM((1, half), f32), pltpu.VMEM((rep_n, 1, half), f32),
            dma((3,)), dma, dma((8,)),
            dma((own_n, 3)), dma((own_n, 3)), dma((own_n,)), dma((own_n,)),
            dma((rep_n,)), dma((rep_n,)), dma((own_n,)), dma((own_n,)),
            dma((own_n,)), dma((own_n,)), dma((rep_n,)), dma((rep_n,)),
        ],
        compiler_params=pltpu.CompilerParams(
            collective_id=0, has_side_effects=True, vmem_limit_bytes=(63 * 1024 * 1024 - own_n * cap * flat * 2)),
        name="latent_code",
    )(counts[None], sel_index[None], sel_layer[None], block_pool)
    return pl.pallas_call(
        write_out,
        out_shape=tuple(jax.ShapeDtypeStruct(x.shape, x.dtype) for x in (codes, steps, err)),
        in_specs=[vmem] * 3,
        out_specs=(hbm, hbm, hbm),
        scratch_shapes=[dma((own_n + 2,))],
        compiler_params=pltpu.CompilerParams(vmem_limit_bytes=4 * 1024 * 1024),
        name="write_out",
    )(codes, steps, err)


def solution(mesh):
    return jax.shard_map(
        body,
        mesh=mesh,
        in_specs=(
            P(("own", "rep"), None, None),
            P(("own", "rep")),
            P(("own", "rep")),
            P(("own", "rep")),
        ),
        out_specs=(P("own", "rep", None, None, None), P("own", None), P("own", None)),
        check_vma=False,
    )
```

time: 66.3 us -> 62.1 us (0.937)
  Pallas kernels: 64.6 us -> 60.6 us
    pallas_call x1, Pallas kernels: 63.1 us -> 59.1 us  [body(): pl.pallas_call(functools.partial(kernel, own_n, rep_n, cap), out_shape=(p...]
where the time goes in v1:
time: 62.1 us; the launch traced here: 61.9 us
  Pallas kernels  60.6 us (98%)
  between operations  1.29 us (2%)
    pallas_call x1, Pallas kernels, body(): pl.pallas_call(functools.partial(kernel, own_n, rep_n, cap), out_shape=(p...  59.1 us
    pallas_call x1, Pallas kernels, body(): pl.pallas_call(write_out, out_shape=tuple((jax.ShapeDtypeStruct(x.shape,...  1.49 us

profile of v1, /device:TPU:8, one launch (start us, length us, event | category | flops | bytes accessed | tf_op | source)
XLA Modules:
  0.0 61.9 jit_solution(15291740219998856300)
XLA Ops:
  1.3 59.1 %latent_code.1 = (bf16[1,1,8,8,18432]{4,3,2,1,0:T(8,128)(2,1)S(1)}, f32[1,288]{1,0:T(1,128)S(1)}, f32[1,288]{1,0:T(1,128)S(1)}) custom-call(s32[1,1]{1,0:T(1,128)} %bitcast.3.live_hbm, s32[1,32]{1,0:T(1,128)} %bitcast.4, s32[1,32]{1,0:T(1,128)} %bitcast.5, bf16[64,64,576]{2,1,0:T(8,128)(2,1)} %pool_ref.1), custom_call_target="tpu_custom_call" | custom-call | tf_op jit(solution)/shard_map/latent_code/pallas_call | solution.py:330
  60.4 1.5 %write_out.1 = (bf16[1,1,8,8,18432]{4,3,2,1,0:T(8,128)(2,1)}, f32[1,288]{1,0:T(1,128)}, f32[1,288]{1,0:T(1,128)}) custom-call(bf16[1,1,8,8,18432]{4,3,2,1,0:T(8,128)(2,1)S(1)} %get-tuple-element.6.codes_v, f32[1,288]{1,0:T(1,128)S(1)} %get-tuple-element.7.steps_v, f32[1,288]{1,0:T(1,128)S(1)} %get-tuple-element.8.err_v), custom_call_target="tpu_custom_call" | custom-call | tf_op jit(solution)/shard_map/write_out/pallas_call | solution.py:361

commit v2 on v1

v2 whole, which is shorter than its diff:
```python
import functools
import math

import jax
import jax.numpy as jnp
from jax import lax
from jax.experimental import pallas as pl
from jax.experimental.pallas import tpu as pltpu
from jax.sharding import PartitionSpec as P

SLICES = 2
LANES = 128
PIECES = 8
headroom = 0.5


def ring_place(layer, layers):
    odd = layer % 2
    return odd * ((layer + 1) // 2) + (1 - odd) * lax.rem(layers - layer // 2, layers)


def ring_layer(place, layers):
    near = jnp.maximum(2 * place - 1, 0)
    return jnp.where(place <= layers // 2, near, 2 * (layers - place))


def partner_layer(my_layer, layers, k):
    return ring_layer(lax.rem(ring_place(my_layer, layers) + k, layers), layers)


def fill_slots(live, index_row, layer_row, table, layers, cap, empty):
    n_select = index_row.shape[1]
    is_live = lax.broadcasted_iota(jnp.int32, (1, n_select), 1) < live
    before = lax.broadcasted_iota(jnp.int32, (n_select, n_select), 0)
    after = lax.broadcasted_iota(jnp.int32, (n_select, n_select), 1)
    earlier = jnp.where(before < after, 1.0, 0.0)
    wanted = lax.broadcasted_iota(jnp.int32, (layers, n_select), 0)
    matches = jnp.where((layer_row == wanted) & is_live, 1.0, 0.0)
    ranking = jnp.dot(matches, earlier, preferred_element_type=jnp.float32)
    slot = lax.broadcasted_iota(jnp.int32, (cap, n_select), 0).astype(jnp.float32)
    shifted = index_row.astype(jnp.float32) - float(empty)
    for layer in range(layers):
        hit = (ranking[layer:layer + 1] == slot) & (matches[layer:layer + 1] > 0.5)
        found = jnp.sum(jnp.where(hit, shifted, 0.0), axis=1, keepdims=True) + float(empty)
        table[layer * cap:(layer + 1) * cap, :] = jnp.broadcast_to(found, (cap, LANES)).astype(jnp.int32)


def kernel(own_n, rep_n, cap, live_ref, index_hbm, layer_hbm, pool_ref, codes_ref, steps_ref, err_ref,
           sel_v, table, slots, pool_a, pool_b, stage, send, recv, pk_send, pk_recv, pk_rep,
           st_recv, pe_send, pe_recv, er_rep, mine,
           sel_sem, table_sem, pool_sem, send_sem, recv_sem, small_send, small_recv):
    rows, tokens, width = pool_ref.shape
    half = width // SLICES
    group = LANES // math.gcd(half, LANES)
    period = group * half
    loops = tokens // group
    layers = own_n // SLICES
    me = lax.axis_index("own")
    rep = lax.axis_index("rep")
    my_layer = me // SLICES
    my_slice = me % SLICES
    tiles = stage.shape[0]
    denominator = float(own_n * rep_n * cap * tokens)
    f32 = jnp.float32
    early = pool_a.shape[1]

    sels = [pltpu.make_async_copy(index_hbm, sel_v.at[0], sel_sem),
            pltpu.make_async_copy(layer_hbm, sel_v.at[1], sel_sem)]
    for sel in sels:
        sel.start()
    barrier = pltpu.get_barrier_semaphore()
    for k in range(1, own_n):
        pl.semaphore_signal(barrier, inc=1, device_id={"own": lax.rem(me + k, own_n)},
                            device_id_type=pl.DeviceIdType.MESH)
    for k in range(1, rep_n):
        pl.semaphore_signal(barrier, inc=1, device_id={"rep": lax.rem(rep + k, rep_n)},
                            device_id_type=pl.DeviceIdType.MESH)
    for pool, start, sem in ((pool_a, 0, pool_sem.at[0]), (pool_b, early, pool_sem.at[1])):
        for p in range(PIECES):
            here = pl.ds(p * (rows // PIECES), rows // PIECES)
            pltpu.make_async_copy(pool_ref.at[here, start:start + pool.shape[1]], pool.at[here], sem).start()

    def load_wait(pool, sem):
        pltpu.make_async_copy(pool_ref.at[:, 0:pool.shape[1]], pool.at[pl.ds(0, rows)], sem).wait()

    pool_a[rows] = jnp.zeros(pool_a.shape[1:], pool_a.dtype)
    pool_b[rows] = jnp.zeros(pool_b.shape[1:], pool_b.dtype)
    pltpu.make_async_copy(sel_v, sel_v, sel_sem).wait()
    fill_slots(live_ref[0], sel_v[0], sel_v[1], table, layers, cap, rows)
    to_scalars = pltpu.make_async_copy(table, slots, table_sem)
    to_scalars.start()
    to_scalars.wait()
    load_wait(pool_a, pool_sem.at[0])

    def row_of(slot):
        return jnp.minimum(jnp.maximum(slots[slot, 0], 0), rows)

    def layer_peak(layer, carry):
        best = [jnp.zeros(pool.shape[1:], pool.dtype) for pool in (pool_a, pool_b)]
        for c in range(cap):
            row = row_of(layer * cap + c)
            best = [jnp.maximum(b, jnp.abs(pool[row])) for b, pool in zip(best, (pool_a, pool_b))]
        tops = [jnp.max(b.astype(f32), axis=0, keepdims=True) for b in best]
        top = jnp.maximum(tops[0], tops[1])
        for part in range(SLICES):
            pk_send[layer * SLICES + part] = top[:, part * half:(part + 1) * half]
        return carry

    def own_copy(src, dst, s_sem, r_sem, peer):
        return pltpu.make_async_remote_copy(
            src_ref=src, dst_ref=dst, send_sem=s_sem, recv_sem=r_sem,
            device_id={"own": peer}, device_id_type=pl.DeviceIdType.MESH)

    def rep_copy(src, dst, r_sem, peer):
        return pltpu.make_async_remote_copy(
            src_ref=src, dst_ref=dst, send_sem=small_send, recv_sem=r_sem,
            device_id={"rep": peer}, device_id_type=pl.DeviceIdType.MESH)

    def rep_share(table, r_sem):
        for k in range(1, rep_n):
            rep_copy(table.at[rep], table.at[rep], r_sem, lax.rem(rep + k, rep_n)).start()

    def arrived(dst, count, r_sem):
        own_copy(dst.at[pl.ds(0, count)], dst.at[pl.ds(0, count)], small_send, r_sem, lax.rem(me + 1, own_n)).wait_recv()

    eighth = loops // 8
    first, second = (0, eighth), (eighth, 2 * eighth)
    third, rest = (3 * eighth, 3 * eighth), (6 * eighth, loops - 6 * eighth)
    all_cols = (0, loops)

    def block_copy(peer, landing, cols, into, r_sem):
        lanes = pl.ds(cols[0] * period, cols[1] * period)
        return own_copy(send.at[peer, :, lanes], into.at[landing, :, lanes], send_sem, r_sem, peer)

    def flatten_layer(layer, cols):
        start, count = cols
        ranges = []
        for pool, begin in ((pool_a, 0), (pool_b, early)):
            t0, t1 = max(start * group, begin), min((start + count) * group, begin + pool.shape[1])
            if t0 < t1:
                ranges.append((pool, begin, t0, t1))
        for c in range(cap):
            row = row_of(layer * cap + c)
            for pool, begin, t0, t1 in ranges:
                block = pool[row, t0 - begin:t1 - begin, :].astype(f32)
                for q in range(tiles):
                    lo, hi = q * LANES, min(width, (q + 1) * LANES)
                    stage[q, c * tokens + t0:c * tokens + t1, 0:hi - lo] = block[:, lo:hi]

        def flatten(i, carry):
            rows_of = [
                jnp.concatenate(
                    [stage[q, pl.ds(i * group + j, cap, stride=tokens), :] for q in range(tiles)], axis=1)
                for j in range(group)
            ]
            for part in range(SLICES):
                joined = jnp.concatenate([r[:, part * half:(part + 1) * half] for r in rows_of], axis=1)
                at = pl.multiple_of(i * period, period)
                send[layer * SLICES + part, :, pl.ds(at, period)] = joined.astype(send.dtype)
            return carry

        lax.fori_loop(start, start + count, flatten, 0)

    def owner(layer, part):
        return layer * SLICES + lax.rem(my_slice + part, SLICES)

    across_first = list(range(1, SLICES)) + [0]
    order = [k for k in range(1, layers) if k != layers // 2]
    last = partner_layer(my_layer, layers, layers // 2)
    to_layer = [partner_layer(my_layer, layers, k) for k in order]
    from_layer = [partner_layer(my_layer, layers, layers - k) for k in order]
    mine_sem, last_sem = recv_sem.at[layers - 2], recv_sem.at[layers - 1]
    pk_sem, pr_sem, st_sem, pe_sem, er_sem = (small_recv.at[i] for i in range(5))

    def send_blocks(i, cols):
        for part in across_first:
            block_copy(owner(to_layer[i], part), me, cols, recv, recv_sem.at[i]).start()

    flatten_layer(to_layer[0], first)
    pl.semaphore_wait(barrier, own_n - 1 + rep_n - 1)
    send_blocks(0, first)
    load_wait(pool_b, pool_sem.at[1])
    lax.fori_loop(0, layers, layer_peak, 0, unroll=4)
    for k in range(1, own_n):
        peer = lax.rem(me + k, own_n)
        own_copy(pk_send.at[peer], pk_recv.at[me], small_send, pk_sem, peer).start()
    for cols in (second, third):
        flatten_layer(to_layer[0], cols)
        send_blocks(0, cols)
    flatten_layer(to_layer[0], rest)
    for i in range(1, layers - 2):
        flatten_layer(to_layer[i], all_cols)
    flatten_layer(last, all_cols)

    arrived(pk_recv, own_n - 1, pk_sem)
    best = pk_send[me]
    for k in range(1, own_n):
        best = jnp.maximum(best, pk_recv[lax.rem(me + k, own_n)])
    pk_rep[rep] = best
    rep_share(pk_rep, pr_sem)
    flatten_layer(my_layer, all_cols)
    arrived(pk_rep, rep_n - 1, pr_sem)
    for k in range(1, rep_n):
        best = jnp.maximum(best, pk_rep[lax.rem(rep + k, rep_n)])

    step = headroom * jnp.maximum(best, 1.0) / 127.0
    steps_ref[...] = step
    mine[...] = step
    for part in across_first:
        own_copy(mine, st_recv.at[me], small_send, st_sem, owner(last, part)).start()
    for i in range(1, layers - 2):
        send_blocks(i, all_cols)
    send_blocks(0, rest)
    for part in range(1, SLICES):
        block_copy(owner(my_layer, part), me, all_cols, recv, mine_sem).start()

    def wide(row):
        return jnp.broadcast_to(jnp.concatenate([row] * group, axis=1), (cap, period))

    def encode(source, target, src, one_step, total):
        step_wide = wide(one_step)
        inv_wide = wide(1.0 / one_step)

        def one(i, total):
            lanes = pl.ds(pl.multiple_of(i * period, period), period)
            x = source[src, :, lanes].astype(f32)
            y = jnp.clip(x * inv_wide, -127.0, 127.0).astype(codes_ref.dtype)
            target[src, :, lanes] = y
            diff = x - y.astype(f32) * step_wide
            return total + diff * diff
        return lax.fori_loop(0, loops, one, total)

    def fold(total):
        row = jnp.sum(total, axis=0, keepdims=True)
        folded = row[:, :half]
        for j in range(1, group):
            folded = folded + row[:, j * half:(j + 1) * half]
        return folded

    def blocks_arrived(count, r_sem):
        arrived(recv, count, r_sem)

    zero = jnp.zeros((cap, period), f32)
    codes_at = codes_ref.at[0, 0]
    total = encode(send, codes_at, me, step, zero)

    arrived(st_recv, SLICES, st_sem)
    for part in across_first:
        peer = owner(last, part)
        pe_send[peer] = fold(encode(send, send, peer, st_recv[peer], zero))
        own_copy(pe_send.at[peer], pe_recv.at[me], small_send, pe_sem, peer).start()
    for part in across_first:
        block_copy(owner(last, part), me, all_cols, codes_at, last_sem).start()

    blocks_arrived(SLICES, recv_sem.at[0])
    for part in across_first:
        total = encode(recv, codes_at, owner(from_layer[0], part), step, total)
    blocks_arrived(SLICES - 1, mine_sem)
    for part in range(1, SLICES):
        total = encode(recv, codes_at, owner(my_layer, part), step, total)
    for i in range(1, layers - 2):
        blocks_arrived(SLICES, recv_sem.at[i])
        for part in across_first:
            total = encode(recv, codes_at, owner(from_layer[i], part), step, total)

    error = fold(total)
    arrived(pe_recv, SLICES, pe_sem)
    for part in across_first:
        error = error + pe_recv[owner(last, part)]
    er_rep[rep] = error
    rep_share(er_rep, er_sem)
    arrived(er_rep, rep_n - 1, er_sem)
    whole = er_rep[0]
    for k in range(1, rep_n):
        whole = whole + er_rep[k]
    err_ref[...] = whole / (step * step * denominator)

    peer = lax.rem(me + 1, own_n)
    sent = own_n - 1 + 2 * (rep_n - 1) + 2 * SLICES
    many = pk_send.at[pl.ds(0, sent)]
    own_copy(many, many, small_send, last_sem, peer).wait_send()
    own_copy(send.at[pl.ds(0, own_n - 1)], recv.at[pl.ds(0, own_n - 1)], send_sem, last_sem, peer).wait_send()
    blocks_arrived(SLICES, last_sem)


def write_out(codes_v, steps_v, err_v, codes_ref, steps_ref, err_ref, sem, small_sem):
    own_n = codes_v.shape[2]
    for src in range(own_n):
        pltpu.make_async_copy(codes_v.at[0, 0, src], codes_ref.at[0, 0, src], sem).start()
    smalls = [pltpu.make_async_copy(steps_v, steps_ref, small_sem.at[0]),
              pltpu.make_async_copy(err_v, err_ref, small_sem.at[1])]
    for small in smalls:
        small.start()
    pltpu.make_async_copy(codes_v, codes_ref, sem).wait()
    for small in smalls:
        small.wait()


def body(block_pool, sel_index, sel_layer, counts):
    own_n = lax.axis_size("own")
    rep_n = lax.axis_size("rep")
    cap = sel_index.shape[0] // 4
    rows, tokens, width = block_pool.shape
    n_select = sel_index.shape[0]
    half = width // SLICES
    flat = tokens * half
    layers = own_n // SLICES
    f32, i32 = jnp.float32, jnp.int32
    dma = pltpu.SemaphoreType.DMA
    dtype = block_pool.dtype

    def row(n):
        return pltpu.VMEM((n, 1, half), f32)

    hbm = pl.BlockSpec(memory_space=pltpu.HBM)
    vmem = pl.BlockSpec(memory_space=pltpu.VMEM)
    codes, steps, err = pl.pallas_call(
        functools.partial(kernel, own_n, rep_n, cap),
        out_shape=(
            pltpu.VMEM((1, 1, own_n, cap, flat), dtype),
            pltpu.VMEM((1, half), f32),
            pltpu.VMEM((1, half), f32),
        ),
        in_specs=[pl.BlockSpec(memory_space=pltpu.SMEM)] + [hbm] * 3,
        out_specs=(vmem,) * 3,
        scratch_shapes=[
            pltpu.VMEM((2, 1, n_select), i32),
            pltpu.VMEM((layers * cap, LANES), i32),
            pltpu.SMEM((layers * cap, LANES), i32),
            pltpu.VMEM((rows + 1, tokens // 4, width), dtype),
            pltpu.VMEM((rows + 1, tokens - tokens // 4, width), dtype),
            pltpu.VMEM((pl.cdiv(width, LANES), cap * tokens, LANES), f32),
            pltpu.VMEM((own_n, cap, flat), dtype),
            pltpu.VMEM((own_n, cap, flat), dtype),
            row(own_n + 2 * rep_n + 2 * SLICES), row(own_n), row(rep_n),
            row(own_n), row(own_n), row(own_n), row(rep_n), pltpu.VMEM((1, half), f32),
            dma, dma, dma((2,)), dma, dma((layers,)), dma, dma((5,)),
        ],
        compiler_params=pltpu.CompilerParams(
            collective_id=0, has_side_effects=True, vmem_limit_bytes=(63 * 1024 * 1024 - own_n * cap * flat * 2)),
        name="latent_code",
    )(counts, sel_index[None], sel_layer[None], block_pool)
    return pl.pallas_call(
        write_out,
        out_shape=tuple(jax.ShapeDtypeStruct(x.shape, x.dtype) for x in (codes, steps, err)),
        in_specs=[vmem] * 3,
        out_specs=(hbm, hbm, hbm),
        scratch_shapes=[dma, dma((2,))],
        compiler_params=pltpu.CompilerParams(vmem_limit_bytes=4 * 1024 * 1024),
        name="write_out",
    )(codes, steps, err)


def solution(mesh):
    return jax.shard_map(
        body,
        mesh=mesh,
        in_specs=(
            P(("own", "rep"), None, None),
            P(("own", "rep")),
            P(("own", "rep")),
            P(("own", "rep")),
        ),
        out_specs=(P("own", "rep", None, None, None), P("own", None), P("own", None)),
        check_vma=False,
    )
```

time: 62.1 us -> 59 us (0.950)
  Pallas kernels: 60.6 us -> 57.5 us
    pallas_call x1, Pallas kernels: 59.1 us -> 56.1 us  [body(): pl.pallas_call(functools.partial(kernel, own_n, rep_n, cap), out_shape=(p...]
where the time goes in v2:
time: 59 us; the launch traced here: 58.8 us
  Pallas kernels  57.5 us (97%)
  between operations  1.29 us (2%)
    pallas_call x1, Pallas kernels, body(): pl.pallas_call(functools.partial(kernel, own_n, rep_n, cap), out_shape=(p...  56.1 us
    pallas_call x1, Pallas kernels, body(): pl.pallas_call(write_out, out_shape=tuple((jax.ShapeDtypeStruct(x.shape,...  1.43 us

profile of v2, /device:TPU:8, one launch (start us, length us, event | category | flops | bytes accessed | tf_op | source)
XLA Modules:
  0.0 58.8 jit_solution(5045546087590008865)
XLA Ops:
  1.3 56.1 %latent_code.1 = (bf16[1,1,8,8,18432]{4,3,2,1,0:T(8,128)(2,1)S(1)}, f32[1,288]{1,0:T(1,128)S(1)}, f32[1,288]{1,0:T(1,128)S(1)}) custom-call(s32[1]{0:T(128)S(6)} %copy.7.live_ref, s32[1,32]{1,0:T(1,128)} %bitcast.2, s32[1,32]{1,0:T(1,128)} %bitcast.3, bf16[64,64,576]{2,1,0:T(8,128)(2,1)} %pool_ref.1), custom_call_target="tpu_custom_call" | custom-call | tf_op jit(solution)/shard_map/latent_code/pallas_call | solution.py:317
  57.4 1.4 %write_out.1 = (bf16[1,1,8,8,18432]{4,3,2,1,0:T(8,128)(2,1)}, f32[1,288]{1,0:T(1,128)}, f32[1,288]{1,0:T(1,128)}) custom-call(bf16[1,1,8,8,18432]{4,3,2,1,0:T(8,128)(2,1)S(1)} %get-tuple-element.6.codes_v, f32[1,288]{1,0:T(1,128)S(1)} %get-tuple-element.7.steps_v, f32[1,288]{1,0:T(1,128)S(1)} %get-tuple-element.8.err_v), custom_call_target="tpu_custom_call" | custom-call | tf_op jit(solution)/shard_map/write_out/pallas_call | solution.py:343

commit v3 on v2

--- a/solution.py
+++ b/solution.py
@@ -48,7 +48,7 @@
 def kernel(own_n, rep_n, cap, live_ref, index_hbm, layer_hbm, pool_ref, codes_ref, steps_ref, err_ref,
            sel_v, table, slots, pool_a, pool_b, stage, send, recv, pk_send, pk_recv, pk_rep,
            st_recv, pe_send, pe_recv, er_rep, mine,
-           sel_sem, table_sem, pool_sem, send_sem, recv_sem, small_send, small_recv):
+           sel_sem, table_sem, pool_sem, send_sem, recv_sem, small_send, small_recv, late_sem):
     rows, tokens, width = pool_ref.shape
     half = width // SLICES
     group = LANES // math.gcd(half, LANES)
@@ -69,12 +69,24 @@
     for sel in sels:
         sel.start()
     barrier = pltpu.get_barrier_semaphore()
-    for k in range(1, own_n):
-        pl.semaphore_signal(barrier, inc=1, device_id={"own": lax.rem(me + k, own_n)},
-                            device_id_type=pl.DeviceIdType.MESH)
+    is_inner = (my_layer > 0) & (my_layer < layers - 1)
+
+    def greet(sem, axis, index):
+        pl.semaphore_signal(sem, inc=1, device_id={axis: index}, device_id_type=pl.DeviceIdType.MESH)
+
+    @pl.when(my_layer < layers - 1)
+    def _():
+        for k in range(1, own_n):
+            greet(barrier, "own", lax.rem(me + k, own_n))
+
+    @pl.when(my_layer == layers - 1)
+    def _():
+        for part in range(SLICES):
+            greet(barrier, "own", part)
+        for part in range(1, SLICES):
+            greet(barrier, "own", my_layer * SLICES + lax.rem(my_slice + part, SLICES))
     for k in range(1, rep_n):
-        pl.semaphore_signal(barrier, inc=1, device_id={"rep": lax.rem(rep + k, rep_n)},
-                            device_id_type=pl.DeviceIdType.MESH)
+        greet(barrier, "rep", lax.rem(rep + k, rep_n))
     for pool, start, sem in ((pool_a, 0, pool_sem.at[0]), (pool_b, early, pool_sem.at[1])):
         for p in range(PIECES):
             here = pl.ds(p * (rows // PIECES), rows // PIECES)
@@ -124,8 +136,10 @@
         own_copy(dst.at[pl.ds(0, count)], dst.at[pl.ds(0, count)], small_send, r_sem, lax.rem(me + 1, own_n)).wait_recv()
 
     eighth = loops // 8
-    first, second = (0, eighth), (eighth, 2 * eighth)
-    third, rest = (3 * eighth, 3 * eighth), (6 * eighth, loops - 6 * eighth)
+    raw = ((0, eighth), (eighth, eighth))
+    coded = (2 * eighth, loops - 2 * eighth)
+    early_cols = ((0, 3 * eighth), (3 * eighth, 3 * eighth))
+    held = (6 * eighth, loops - 6 * eighth)
     all_cols = (0, loops)
 
     def block_copy(peer, landing, cols, into, r_sem):
@@ -169,28 +183,46 @@
     last = partner_layer(my_layer, layers, layers // 2)
     to_layer = [partner_layer(my_layer, layers, k) for k in order]
     from_layer = [partner_layer(my_layer, layers, layers - k) for k in order]
-    mine_sem, last_sem = recv_sem.at[layers - 2], recv_sem.at[layers - 1]
+    mine_sem, last_sem, raw_sem = (recv_sem.at[layers - 2 + i] for i in range(3))
     pk_sem, pr_sem, st_sem, pe_sem, er_sem = (small_recv.at[i] for i in range(5))
 
     def send_blocks(i, cols):
         for part in across_first:
             block_copy(owner(to_layer[i], part), me, cols, recv, recv_sem.at[i]).start()
 
-    flatten_layer(to_layer[0], first)
-    pl.semaphore_wait(barrier, own_n - 1 + rep_n - 1)
-    send_blocks(0, first)
+    def send_last(cols, into, r_sem):
+        for part in across_first:
+            block_copy(owner(last, part), me, cols, into, r_sem).start()
+
+    flatten_layer(last, raw[0])
+    pl.semaphore_wait(barrier, own_n - 1 + rep_n - 1 - jnp.where(is_inner, SLICES, 0))
+    send_last(raw[0], recv, raw_sem)
+
+    @pl.when(my_layer == 0)
+    def _():
+        for layer in range(1, layers - 1):
+            greet(late_sem, "own", layer * SLICES + my_slice)
+
+    flatten_layer(last, raw[1])
+    send_last(raw[1], recv, raw_sem)
     load_wait(pool_b, pool_sem.at[1])
     lax.fori_loop(0, layers, layer_peak, 0, unroll=4)
+    flatten_layer(to_layer[0], early_cols[0])
+
+    @pl.when(is_inner)
+    def _():
+        pl.semaphore_wait(late_sem, 1)
+
     for k in range(1, own_n):
         peer = lax.rem(me + k, own_n)
         own_copy(pk_send.at[peer], pk_recv.at[me], small_send, pk_sem, peer).start()
-    for cols in (second, third):
-        flatten_layer(to_layer[0], cols)
-        send_blocks(0, cols)
-    flatten_layer(to_layer[0], rest)
+    send_blocks(0, early_cols[0])
+    flatten_layer(to_layer[0], early_cols[1])
+    send_blocks(0, early_cols[1])
+    flatten_layer(to_layer[0], held)
     for i in range(1, layers - 2):
         flatten_layer(to_layer[i], all_cols)
-    flatten_layer(last, all_cols)
+    flatten_layer(last, coded)
 
     arrived(pk_recv, own_n - 1, pk_sem)
     best = pk_send[me]
@@ -210,14 +242,14 @@
         own_copy(mine, st_recv.at[me], small_send, st_sem, owner(last, part)).start()
     for i in range(1, layers - 2):
         send_blocks(i, all_cols)
-    send_blocks(0, rest)
+    send_blocks(0, held)
     for part in range(1, SLICES):
         block_copy(owner(my_layer, part), me, all_cols, recv, mine_sem).start()
 
     def wide(row):
         return jnp.broadcast_to(jnp.concatenate([row] * group, axis=1), (cap, period))
 
-    def encode(source, target, src, one_step, total):
+    def encode(source, target, src, one_step, total, cols=all_cols):
         step_wide = wide(one_step)
         inv_wide = wide(1.0 / one_step)
 
@@ -228,7 +260,7 @@
             target[src, :, lanes] = y
             diff = x - y.astype(f32) * step_wide
             return total + diff * diff
-        return lax.fori_loop(0, loops, one, total)
+        return lax.fori_loop(cols[0], cols[0] + cols[1], one, total)
 
     def fold(total):
         row = jnp.sum(total, axis=0, keepdims=True)
@@ -237,8 +269,9 @@
             folded = folded + row[:, j * half:(j + 1) * half]
         return folded
 
-    def blocks_arrived(count, r_sem):
-        arrived(recv, count, r_sem)
+    def blocks_arrived(count, r_sem, n_loops=loops):
+        some = recv.at[pl.ds(0, count), :, pl.ds(0, n_loops * period)]
+        own_copy(some, some, small_send, r_sem, lax.rem(me + 1, own_n)).wait_recv()
 
     zero = jnp.zeros((cap, period), f32)
     codes_at = codes_ref.at[0, 0]
@@ -247,11 +280,13 @@
     arrived(st_recv, SLICES, st_sem)
     for part in across_first:
         peer = owner(last, part)
-        pe_send[peer] = fold(encode(send, send, peer, st_recv[peer], zero))
+        pe_send[peer] = fold(encode(send, send, peer, st_recv[peer], zero, coded))
         own_copy(pe_send.at[peer], pe_recv.at[me], small_send, pe_sem, peer).start()
+    send_last(coded, codes_at, last_sem)
+
+    blocks_arrived(SLICES, raw_sem, coded[0])
     for part in across_first:
-        block_copy(owner(last, part), me, all_cols, codes_at, last_sem).start()
-
+        total = encode(recv, codes_at, owner(last, part), step, total, (0, coded[0]))
     blocks_arrived(SLICES, recv_sem.at[0])
     for part in across_first:
         total = encode(recv, codes_at, owner(from_layer[0], part), step, total)
@@ -280,7 +315,7 @@
     many = pk_send.at[pl.ds(0, sent)]
     own_copy(many, many, small_send, last_sem, peer).wait_send()
     own_copy(send.at[pl.ds(0, own_n - 1)], recv.at[pl.ds(0, own_n - 1)], send_sem, last_sem, peer).wait_send()
-    blocks_arrived(SLICES, last_sem)
+    blocks_arrived(SLICES, last_sem, coded[1])
 
 
 def write_out(codes_v, steps_v, err_v, codes_ref, steps_ref, err_ref, sem, small_sem):
@@ -334,7 +369,7 @@
             pltpu.VMEM((own_n, cap, flat), dtype),
             row(own_n + 2 * rep_n + 2 * SLICES), row(own_n), row(rep_n),
             row(own_n), row(own_n), row(own_n), row(rep_n), pltpu.VMEM((1, half), f32),
-            dma, dma, dma((2,)), dma, dma((layers,)), dma, dma((5,)),
+            dma, dma, dma((2,)), dma, dma((layers + 1,)), dma, dma((5,)), pltpu.SemaphoreType.REGULAR,
         ],
         compiler_params=pltpu.CompilerParams(
             collective_id=0, has_side_effects=True, vmem_limit_bytes=(63 * 1024 * 1024 - own_n * cap * flat * 2)),

time: 59 us -> 58.4 us (0.990)
  Pallas kernels: 57.5 us -> 56.9 us
    pallas_call x1, Pallas kernels: 56.1 us -> 55.5 us  [body(): pl.pallas_call(functools.partial(kernel, own_n, rep_n, cap), out_shape=(p...]
where the time goes in v3:
time: 58.4 us; the launch traced here: 58.2 us
  Pallas kernels  56.9 us (97%)
  between operations  1.29 us (2%)
    pallas_call x1, Pallas kernels, body(): pl.pallas_call(functools.partial(kernel, own_n, rep_n, cap), out_shape=(p...  55.5 us
    pallas_call x1, Pallas kernels, body(): pl.pallas_call(write_out, out_shape=tuple((jax.ShapeDtypeStruct(x.shape,...  1.43 us

profile of v3, /device:TPU:8, one launch (start us, length us, event | category | flops | bytes accessed | tf_op | source)
XLA Modules:
  0.0 58.2 jit_solution(12969561658757907760)
XLA Ops:
  1.3 55.5 %latent_code.1 = (bf16[1,1,8,8,18432]{4,3,2,1,0:T(8,128)(2,1)S(1)}, f32[1,288]{1,0:T(1,128)S(1)}, f32[1,288]{1,0:T(1,128)S(1)}) custom-call(s32[1]{0:T(128)S(6)} %copy.7.live_ref, s32[1,32]{1,0:T(1,128)} %bitcast.2, s32[1,32]{1,0:T(1,128)} %bitcast.3, bf16[64,64,576]{2,1,0:T(8,128)(2,1)} %pool_ref.1), custom_call_target="tpu_custom_call" | custom-call | tf_op jit(solution)/shard_map/latent_code/pallas_call | solution.py:352
  56.8 1.4 %write_out.1 = (bf16[1,1,8,8,18432]{4,3,2,1,0:T(8,128)(2,1)}, f32[1,288]{1,0:T(1,128)}, f32[1,288]{1,0:T(1,128)}) custom-call(bf16[1,1,8,8,18432]{4,3,2,1,0:T(8,128)(2,1)S(1)} %get-tuple-element.6.codes_v, f32[1,288]{1,0:T(1,128)S(1)} %get-tuple-element.7.steps_v, f32[1,288]{1,0:T(1,128)S(1)} %get-tuple-element.8.err_v), custom_call_target="tpu_custom_call" | custom-call | tf_op jit(solution)/shard_map/write_out/pallas_call | solution.py:378

commit v4 on v3

--- a/solution.py
+++ b/solution.py
@@ -39,10 +39,16 @@
     ranking = jnp.dot(matches, earlier, preferred_element_type=jnp.float32)
     slot = lax.broadcasted_iota(jnp.int32, (cap, n_select), 0).astype(jnp.float32)
     shifted = index_row.astype(jnp.float32) - float(empty)
+    place = lax.broadcasted_iota(jnp.int32, (cap, table.shape[1]), 1)
+    spread = jnp.zeros((cap, table.shape[1]), jnp.float32)
     for layer in range(layers):
         hit = (ranking[layer:layer + 1] == slot) & (matches[layer:layer + 1] > 0.5)
         found = jnp.sum(jnp.where(hit, shifted, 0.0), axis=1, keepdims=True) + float(empty)
-        table[layer * cap:(layer + 1) * cap, :] = jnp.broadcast_to(found, (cap, LANES)).astype(jnp.int32)
+        here = place == layer * cap + lax.broadcasted_iota(jnp.int32, place.shape, 0)
+        spread = spread + jnp.where(here, found, 0.0)
+    row = jnp.sum(spread, axis=0, keepdims=True)
+    table[...] = row.astype(jnp.int32)
+    return row
 
 
 def kernel(own_n, rep_n, cap, live_ref, index_hbm, layer_hbm, pool_ref, codes_ref, steps_ref, err_ref,
@@ -98,14 +104,19 @@
     pool_a[rows] = jnp.zeros(pool_a.shape[1:], pool_a.dtype)
     pool_b[rows] = jnp.zeros(pool_b.shape[1:], pool_b.dtype)
     pltpu.make_async_copy(sel_v, sel_v, sel_sem).wait()
-    fill_slots(live_ref[0], sel_v[0], sel_v[1], table, layers, cap, rows)
+    filled = fill_slots(live_ref[0], sel_v[0], sel_v[1], table, layers, cap, rows)
     to_scalars = pltpu.make_async_copy(table, slots, table_sem)
     to_scalars.start()
-    to_scalars.wait()
+    last = partner_layer(my_layer, layers, layers // 2)
+    place = lax.broadcasted_iota(jnp.int32, filled.shape, 1)
+    first_rows = []
+    for c in range(cap):
+        row = jnp.sum(jnp.where(place == last * cap + c, filled, 0.0)).astype(jnp.int32)
+        first_rows.append(jnp.minimum(jnp.maximum(row, 0), rows))
     load_wait(pool_a, pool_sem.at[0])
 
     def row_of(slot):
-        return jnp.minimum(jnp.maximum(slots[slot, 0], 0), rows)
+        return jnp.minimum(jnp.maximum(slots[0, slot], 0), rows)
 
     def layer_peak(layer, carry):
         best = [jnp.zeros(pool.shape[1:], pool.dtype) for pool in (pool_a, pool_b)]
@@ -138,7 +149,7 @@
     eighth = loops // 8
     raw = ((0, eighth), (eighth, eighth))
     coded = (2 * eighth, loops - 2 * eighth)
-    early_cols = ((0, 3 * eighth), (3 * eighth, 3 * eighth))
+    early_cols = ((0, eighth), (eighth, 5 * eighth))
     held = (6 * eighth, loops - 6 * eighth)
     all_cols = (0, loops)
 
@@ -146,7 +157,7 @@
         lanes = pl.ds(cols[0] * period, cols[1] * period)
         return own_copy(send.at[peer, :, lanes], into.at[landing, :, lanes], send_sem, r_sem, peer)
 
-    def flatten_layer(layer, cols):
+    def flatten_layer(layer, cols, known=None):
         start, count = cols
         ranges = []
         for pool, begin in ((pool_a, 0), (pool_b, early)):
@@ -154,7 +165,7 @@
             if t0 < t1:
                 ranges.append((pool, begin, t0, t1))
         for c in range(cap):
-            row = row_of(layer * cap + c)
+            row = known[c] if known else row_of(layer * cap + c)
             for pool, begin, t0, t1 in ranges:
                 block = pool[row, t0 - begin:t1 - begin, :].astype(f32)
                 for q in range(tiles):
@@ -180,7 +191,6 @@
 
     across_first = list(range(1, SLICES)) + [0]
     order = [k for k in range(1, layers) if k != layers // 2]
-    last = partner_layer(my_layer, layers, layers // 2)
     to_layer = [partner_layer(my_layer, layers, k) for k in order]
     from_layer = [partner_layer(my_layer, layers, layers - k) for k in order]
     mine_sem, last_sem, raw_sem = (recv_sem.at[layers - 2 + i] for i in range(3))
@@ -194,7 +204,7 @@
         for part in across_first:
             block_copy(owner(last, part), me, cols, into, r_sem).start()
 
-    flatten_layer(last, raw[0])
+    flatten_layer(last, raw[0], first_rows)
     pl.semaphore_wait(barrier, own_n - 1 + rep_n - 1 - jnp.where(is_inner, SLICES, 0))
     send_last(raw[0], recv, raw_sem)
 
@@ -203,11 +213,19 @@
         for layer in range(1, layers - 1):
             greet(late_sem, "own", layer * SLICES + my_slice)
 
+    to_scalars.wait()
     flatten_layer(last, raw[1])
     send_last(raw[1], recv, raw_sem)
     load_wait(pool_b, pool_sem.at[1])
     lax.fori_loop(0, layers, layer_peak, 0, unroll=4)
     flatten_layer(to_layer[0], early_cols[0])
+    is_later = is_inner & (to_layer[0] == layers - 1)
+
+    @pl.when(jnp.logical_not(is_later))
+    def _():
+        send_blocks(0, early_cols[0])
+
+    flatten_layer(to_layer[0], early_cols[1])
 
     @pl.when(is_inner)
     def _():
@@ -216,8 +234,11 @@
     for k in range(1, own_n):
         peer = lax.rem(me + k, own_n)
         own_copy(pk_send.at[peer], pk_recv.at[me], small_send, pk_sem, peer).start()
-    send_blocks(0, early_cols[0])
-    flatten_layer(to_layer[0], early_cols[1])
+
+    @pl.when(is_later)
+    def _():
+        send_blocks(0, early_cols[0])
+
     send_blocks(0, early_cols[1])
     flatten_layer(to_layer[0], held)
     for i in range(1, layers - 2):
@@ -360,8 +381,8 @@
         out_specs=(vmem,) * 3,
         scratch_shapes=[
             pltpu.VMEM((2, 1, n_select), i32),
-            pltpu.VMEM((layers * cap, LANES), i32),
-            pltpu.SMEM((layers * cap, LANES), i32),
+            pltpu.VMEM((1, pl.cdiv(layers * cap, LANES) * LANES), i32),
+            pltpu.SMEM((1, pl.cdiv(layers * cap, LANES) * LANES), i32),
             pltpu.VMEM((rows + 1, tokens // 4, width), dtype),
             pltpu.VMEM((rows + 1, tokens - tokens // 4, width), dtype),
             pltpu.VMEM((pl.cdiv(width, LANES), cap * tokens, LANES), f32),

time: 58.4 us -> 58.4 us (level)
  no operation moved by 1% of the time
where the time goes in v4:
time: 58.4 us; the launch traced here: 58.2 us
  Pallas kernels  56.9 us (97%)
  between operations  1.29 us (2%)
    pallas_call x1, Pallas kernels, body(): pl.pallas_call(functools.partial(kernel, own_n, rep_n, cap), out_shape=(p...  55.5 us
    pallas_call x1, Pallas kernels, body(): pl.pallas_call(write_out, out_shape=tuple((jax.ShapeDtypeStruct(x.shape,...  1.43 us

profile of v4, /device:TPU:8, one launch (start us, length us, event | category | flops | bytes accessed | tf_op | source)
XLA Modules:
  0.0 58.2 jit_solution(15049352941659820007)
XLA Ops:
  1.3 55.5 %latent_code.1 = (bf16[1,1,8,8,18432]{4,3,2,1,0:T(8,128)(2,1)S(1)}, f32[1,288]{1,0:T(1,128)S(1)}, f32[1,288]{1,0:T(1,128)S(1)}) custom-call(s32[1]{0:T(128)S(6)} %copy.7.live_ref, s32[1,32]{1,0:T(1,128)} %bitcast.2, s32[1,32]{1,0:T(1,128)} %bitcast.3, bf16[64,64,576]{2,1,0:T(8,128)(2,1)} %pool_ref.1), custom_call_target="tpu_custom_call" | custom-call | tf_op jit(solution)/shard_map/latent_code/pallas_call | solution.py:373
  56.8 1.4 %write_out.1 = (bf16[1,1,8,8,18432]{4,3,2,1,0:T(8,128)(2,1)}, f32[1,288]{1,0:T(1,128)}, f32[1,288]{1,0:T(1,128)}) custom-call(bf16[1,1,8,8,18432]{4,3,2,1,0:T(8,128)(2,1)S(1)} %get-tuple-element.6.codes_v, f32[1,288]{1,0:T(1,128)S(1)} %get-tuple-element.7.steps_v, f32[1,288]{1,0:T(1,128)S(1)} %get-tuple-element.8.err_v), custom_call_target="tpu_custom_call" | custom-call | tf_op jit(solution)/shard_map/write_out/pallas_call | solution.py:399

commit v5 on v4

--- a/solution.py
+++ b/solution.py
@@ -82,15 +82,20 @@
 
     @pl.when(my_layer < layers - 1)
     def _():
-        for k in range(1, own_n):
-            greet(barrier, "own", lax.rem(me + k, own_n))
+        for k in range(1, layers):
+            for part in range(SLICES):
+                greet(barrier, "own", lax.rem(my_layer + k, layers) * SLICES + part)
 
     @pl.when(my_layer == layers - 1)
     def _():
         for part in range(SLICES):
             greet(barrier, "own", part)
+
+    @pl.when(jnp.logical_not(is_inner))
+    def _():
         for part in range(1, SLICES):
             greet(barrier, "own", my_layer * SLICES + lax.rem(my_slice + part, SLICES))
+
     for k in range(1, rep_n):
         greet(barrier, "rep", lax.rem(rep + k, rep_n))
     for pool, start, sem in ((pool_a, 0, pool_sem.at[0]), (pool_b, early, pool_sem.at[1])):
@@ -147,8 +152,8 @@
         own_copy(dst.at[pl.ds(0, count)], dst.at[pl.ds(0, count)], small_send, r_sem, lax.rem(me + 1, own_n)).wait_recv()
 
     eighth = loops // 8
-    raw = ((0, eighth), (eighth, eighth))
-    coded = (2 * eighth, loops - 2 * eighth)
+    raw = ((0, eighth), (eighth, eighth // 2))
+    coded = (eighth + eighth // 2, loops - eighth - eighth // 2)
     early_cols = ((0, eighth), (eighth, 5 * eighth))
     held = (6 * eighth, loops - 6 * eighth)
     all_cols = (0, loops)
@@ -205,7 +210,7 @@
             block_copy(owner(last, part), me, cols, into, r_sem).start()
 
     flatten_layer(last, raw[0], first_rows)
-    pl.semaphore_wait(barrier, own_n - 1 + rep_n - 1 - jnp.where(is_inner, SLICES, 0))
+    pl.semaphore_wait(barrier, own_n - 1 + rep_n - 1 - jnp.where(is_inner, 2 * SLICES - 1, 0))
     send_last(raw[0], recv, raw_sem)
 
     @pl.when(my_layer == 0)

time: 58.4 us -> 58.3 us (level)
  no operation moved by 1% of the time
where the time goes in v5:
time: 58.3 us; the launch traced here: 58.1 us
  Pallas kernels  56.9 us (98%)
  between operations  1.29 us (2%)
    pallas_call x1, Pallas kernels, body(): pl.pallas_call(functools.partial(kernel, own_n, rep_n, cap), out_shape=(p...  55.4 us
    pallas_call x1, Pallas kernels, body(): pl.pallas_call(write_out, out_shape=tuple((jax.ShapeDtypeStruct(x.shape,...  1.43 us

profile of v5, /device:TPU:8, one launch (start us, length us, event | category | flops | bytes accessed | tf_op | source)
XLA Modules:
  0.0 58.1 jit_solution(5154922607716484427)
XLA Ops:
  1.3 55.4 %latent_code.1 = (bf16[1,1,8,8,18432]{4,3,2,1,0:T(8,128)(2,1)S(1)}, f32[1,288]{1,0:T(1,128)S(1)}, f32[1,288]{1,0:T(1,128)S(1)}) custom-call(s32[1]{0:T(128)S(6)} %copy.7.live_ref, s32[1,32]{1,0:T(1,128)} %bitcast.2, s32[1,32]{1,0:T(1,128)} %bitcast.3, bf16[64,64,576]{2,1,0:T(8,128)(2,1)} %pool_ref.1), custom_call_target="tpu_custom_call" | custom-call | tf_op jit(solution)/shard_map/latent_code/pallas_call | solution.py:378
  56.7 1.4 %write_out.1 = (bf16[1,1,8,8,18432]{4,3,2,1,0:T(8,128)(2,1)}, f32[1,288]{1,0:T(1,128)}, f32[1,288]{1,0:T(1,128)}) custom-call(bf16[1,1,8,8,18432]{4,3,2,1,0:T(8,128)(2,1)S(1)} %get-tuple-element.6.codes_v, f32[1,288]{1,0:T(1,128)S(1)} %get-tuple-element.7.steps_v, f32[1,288]{1,0:T(1,128)S(1)} %get-tuple-element.8.err_v), custom_call_target="tpu_custom_call" | custom-call | tf_op jit(solution)/shard_map/write_out/pallas_call | solution.py:404

commit v6 on v5

--- a/solution.py
+++ b/solution.py
@@ -202,7 +202,7 @@
     pk_sem, pr_sem, st_sem, pe_sem, er_sem = (small_recv.at[i] for i in range(5))
 
     def send_blocks(i, cols):
-        for part in across_first:
+        for part in (across_first if i else across_first[::-1]):
             block_copy(owner(to_layer[i], part), me, cols, recv, recv_sem.at[i]).start()
 
     def send_last(cols, into, r_sem):

time: 58.3 us -> 58.3 us (level)
  no operation moved by 1% of the time
where the time goes in v6:
time: 58.3 us; the launch traced here: 58.1 us
  Pallas kernels  56.9 us (98%)
  between operations  1.29 us (2%)
    pallas_call x1, Pallas kernels, body(): pl.pallas_call(functools.partial(kernel, own_n, rep_n, cap), out_shape=(p...  55.4 us
    pallas_call x1, Pallas kernels, body(): pl.pallas_call(write_out, out_shape=tuple((jax.ShapeDtypeStruct(x.shape,...  1.43 us

profile of v6, /device:TPU:8, one launch (start us, length us, event | category | flops | bytes accessed | tf_op | source)
XLA Modules:
  0.0 58.1 jit_solution(6000391083257743762)
XLA Ops:
  1.3 55.4 %latent_code.1 = (bf16[1,1,8,8,18432]{4,3,2,1,0:T(8,128)(2,1)S(1)}, f32[1,288]{1,0:T(1,128)S(1)}, f32[1,288]{1,0:T(1,128)S(1)}) custom-call(s32[1]{0:T(128)S(6)} %copy.7.live_ref, s32[1,32]{1,0:T(1,128)} %bitcast.2, s32[1,32]{1,0:T(1,128)} %bitcast.3, bf16[64,64,576]{2,1,0:T(8,128)(2,1)} %pool_ref.1), custom_call_target="tpu_custom_call" | custom-call | tf_op jit(solution)/shard_map/latent_code/pallas_call | solution.py:378
  56.7 1.4 %write_out.1 = (bf16[1,1,8,8,18432]{4,3,2,1,0:T(8,128)(2,1)}, f32[1,288]{1,0:T(1,128)}, f32[1,288]{1,0:T(1,128)}) custom-call(bf16[1,1,8,8,18432]{4,3,2,1,0:T(8,128)(2,1)S(1)} %get-tuple-element.6.codes_v, f32[1,288]{1,0:T(1,128)S(1)} %get-tuple-element.7.steps_v, f32[1,288]{1,0:T(1,128)S(1)} %get-tuple-element.8.err_v), custom_call_target="tpu_custom_call" | custom-call | tf_op jit(solution)/shard_map/write_out/pallas_call | solution.py:404
